TPU v7x, 32 devices: a whole 2x2x4 slice. The times are simulated.
32 devices in a mesh: sky: 8 (over y, x, core), tm: 4 (over z).
Axes of the slice: x: 2, y: 2, z: 4, core: 2. Of those that a mesh axis runs over, the one named last changes fastest.
Arguments:
- obs_source: int32 [131072], P(('sky', 'tm')), may hold values from 0 to 1023
- obs_knot: int32 [131072], P(('sky', 'tm')), may hold values from 0 to 2047, as said below
- obs_count: int32 [32], P(('sky', 'tm')), may hold values from 256 to 4096, as said below
- src_design: float32 [5, 131072], P(None, ('sky', 'tm')), may hold values from -3 to 3
- att_design: float32 [4, 131072], P(None, ('sky', 'tm')), may hold values from -6 to 6
- obs_phase: float32 [131072], P(('sky', 'tm')), may hold values from 0 to 1
- obs_value: float32 [131072], P(('sky', 'tm')), may hold values from -6 to 6
- src_prior: float32 [5, 8192], P(None, 'sky'), may hold values from 1 to 16
Outputs:
- att_solution: float32 [4, 4, 2048], P(None, 'tm', 'sky')
- att_residual: float32 [4, 4, 2048], P(None, 'tm', 'sky')
- source_solution: float32 [5, 8192], P(None, 'sky')
Inputs may be any that keep to these rules, and one draw needn't show every extreme that they name: Block b holds the 4096 observation slots o with o // 4096 = b; with i = b // 4 its sources are the sources i * 1024 + obs_source. With j = b % 4 for the observation's block b, its four spline knots are j * 2048 + obs_knot and the next three. In every block, each range of 256 values r * 256 to r * 256 + 255 of obs_knot holds exactly 512 of the block's slots. `obs_count`: each count is 4096 divided by 1, 2, 4, 8 or 16; the live slots of a block are its first ones; some block is full.
All inputs are finite; a program needn't handle non-finite values.
Results may differ from a plain program's by a relative error of at most 0.0001.
Values sent between devices are 32-bit elements; how exact they have to be, the bound alone decides.
A program may use at most 64 MiB of HBM per device.

v0:
```python
import jax
import jax.numpy as jnp
from jax import lax
from jax.sharding import PartitionSpec as P

ITERS = 2
SRC_DEV = 1024
KN_DEV = 256
damping = 0.5
entry_pairs = [(row_at, col_at) for row_at in range(5) for col_at in range(row_at + 1)]


def shifted(value, axis, steps):
    count = lax.axis_size(axis)
    first, last = (max(0, -steps), min(count, count - steps))
    return lax.ppermute(value, axis, [(source, source + steps) for source in range(first, last)])


def spline_taps(phase):
    squared = phase * phase
    cubed = squared * phase
    rest = 1.0 - phase
    return (
        rest * rest * rest / 6.0,
        (3.0 * cubed - 6.0 * squared + 4.0) / 6.0,
        (-3.0 * cubed + 3.0 * squared + 3.0 * phase + 1.0) / 6.0,
        cubed / 6.0,
    )


def factorize(normal):
    factor = {}
    for row_at in range(5):
        for col_at in range(row_at + 1):
            running = normal[row_at, col_at]
            for inner_at in range(col_at):
                running = running - factor[row_at, inner_at] * factor[col_at, inner_at]
            if row_at == col_at:
                factor[row_at, row_at] = jnp.sqrt(running)
            else:
                factor[row_at, col_at] = running / factor[col_at, col_at]
    return factor


def chol_solve(factor, target):
    forward = []
    for row_at in range(5):
        running = target[row_at]
        for inner_at in range(row_at):
            running = running - factor[row_at, inner_at] * forward[inner_at]
        forward.append(running / factor[row_at, row_at])
    result = [None] * 5
    for row_at in reversed(range(5)):
        running = forward[row_at]
        for inner_at in range(row_at + 1, 5):
            running = running - factor[inner_at, row_at] * result[inner_at]
        result[row_at] = running / factor[row_at, row_at]
    return jnp.stack(result)


def source_total(source, rows, count):
    return jnp.zeros((rows.shape[0], count), jnp.float32).at[:, source].add(rows)


def knot_values(padded, knot, design, tap_weights):
    summed = jnp.zeros(knot.shape, jnp.float32)
    for tap_at in range(4):
        picked = jnp.take(padded, knot + tap_at, axis=1)
        summed = summed + tap_weights[tap_at] * jnp.sum(design * picked, axis=0)
    return summed


def knot_total(knot, design, tap_weights, weight_vec, extent):
    summed = jnp.zeros((design.shape[0], extent + 3), jnp.float32)
    for tap_at in range(4):
        summed = summed.at[:, knot + tap_at].add(design * (tap_weights[tap_at] * weight_vec))
    return summed


def eliminate(factor, source, design, values_obs, source_sums):
    solved = chol_solve(factor, [source_sums[row_at] for row_at in range(5)])
    fitted = jnp.sum(design * jnp.take(solved, source, axis=1), axis=0)
    return values_obs - fitted


def shards(
    obs_source, obs_knot, obs_count, src_design, att_design, obs_phase, obs_value, src_prior
):
    sky_count = lax.axis_size("sky")
    seg_knots = KN_DEV * sky_count
    slot_count = obs_source.shape[0]
    live_mask = (jnp.arange(slot_count, dtype=jnp.int32) < obs_count[0]).astype(jnp.float32)
    src_rows = src_design * live_mask
    att_rows = att_design * live_mask
    observed = obs_value * live_mask
    tap_weights = spline_taps(obs_phase)
    products = jnp.stack(
        [src_rows[row_at] * src_rows[col_at] for row_at, col_at in entry_pairs]
        + [src_rows[row_at] * observed for row_at in range(5)]
    )
    sums = lax.psum(source_total(obs_source, products, SRC_DEV), "tm")
    normal = {}
    for entry_at, pair in enumerate(entry_pairs):
        normal[pair] = sums[entry_at] + (src_prior[pair[0]] if pair[0] == pair[1] else 0.0)
    factor = factorize(normal)

    def source_part(values_obs):
        return lax.psum(source_total(obs_source, src_rows * values_obs, SRC_DEV), "tm")

    def along_knots(field):
        segment = lax.all_gather(field, "sky", axis=1, tiled=True)
        next_edge = shifted(segment[:, :3], "tm", -1)
        padded = jnp.concatenate([segment, next_edge], axis=1)
        return knot_values(padded, obs_knot, att_rows, tap_weights)

    def back_to_knots(cleaned):
        summed = knot_total(obs_knot, att_rows, tap_weights, cleaned, seg_knots)
        overflow = shifted(summed[:, seg_knots:], "tm", 1)
        partial_value = summed[:, :seg_knots].at[:, :3].add(overflow)
        return lax.psum_scatter(partial_value, "sky", scatter_dimension=1, tiled=True)

    def norm_sum(partial_value):
        return lax.psum(partial_value, ("sky", "tm"))

    cleaned = eliminate(factor, obs_source, src_rows, observed, sums[15:])
    residual = back_to_knots(cleaned)
    solution = jnp.zeros_like(residual)
    direction = residual
    norm_now = norm_sum(jnp.sum(residual * residual))
    for repeat in range(ITERS):
        image_obs = along_knots(direction)
        cleaned = eliminate(factor, obs_source, src_rows, image_obs, source_part(image_obs))
        mapped = back_to_knots(cleaned) + damping * direction
        alpha_step = norm_now / lax.psum(jnp.sum(direction * mapped), ("sky", "tm"))
        solution = solution + alpha_step * direction
        residual = residual - alpha_step * mapped
        norm_next = norm_sum(jnp.sum(residual * residual))
        direction = residual + norm_next / norm_now * direction
        norm_now = norm_next
    fitted = observed - along_knots(solution)
    source_solution = chol_solve(factor, [row for row in source_part(fitted)])
    return (solution[:, None, :], residual[:, None, :], source_solution)


def solution(mesh):
    placed = (
        P(("sky", "tm")),
        P(("sky", "tm")),
        P(("sky", "tm")),
        P(None, ("sky", "tm")),
        P(None, ("sky", "tm")),
        P(("sky", "tm")),
        P(("sky", "tm")),
        P(None, "sky"),
    )
    return jax.shard_map(
        shards,
        mesh=mesh,
        in_specs=placed,
        out_specs=(P(None, "tm", "sky"), P(None, "tm", "sky"), P(None, "sky")),
        check_vma=False,
    )
```

profile of v0, /device:TPU:0, one launch (start us, length us, event | category | flops | bytes accessed | tf_op | source)
XLA Modules:
  0.0 1068.1 jit_solution(9590675632088410657)
XLA Ops:
  11.7 22.5 %scatter_custom_fusion = f32[20,1024]{0,1:T(8,128)S(1)} fusion(s32[4096]{0:T(1024)S(1)} %get-tuple-element.173, f32[4096,20]{1,0:T(8,128)S(1)} %copy.271, f32[]{:T(128)} %constant.111.clone.1), kind=kCustom, calls=%fused_computation.113 | custom fusion | flops 81920 | bytes 81924 | tf_op jit(solution)/shard_map/scatter-add | solution.py:62
  37.1 35.3 %all-reduce.3.cloned.1.call-done = f32[20,1024]{1,0:T(8,128)} async-done(((f32[20,1024]{1,0:T(8,128)}), f32[20,1024]{1,0:T(8,128)}) %all-reduce.3.cloned.1.call-update) | async-done | bytes 81936 | tf_op jit(solution)/shard_map/psum | solution.py:101
  75.5 14.1 %gather_fusion = f32[4096,5]{1,0:T(8,128)} fusion(f32[5,1024]{0,1:T(8,128)S(1)} %copy.273, s32[4096]{0:T(1024)S(1)} %get-tuple-element.172), kind=kCustom, calls=%fused_computation.clone | custom fusion | bytes 180224 | tf_op jit(solution)/shard_map/jit(_take)/gather | solution.py:82
  92.0 25.3 %scatter_custom_fusion.1 = f32[4,2051]{0,1:T(8,128)S(1)} fusion(s32[4096]{0:T(1024)} %get-tuple-element.168, f32[4096]{0:T(1024)S(1)} %get-tuple-element.159, f32[]{:T(128)} %constant.111.clone.1, f32[4,4096]{0,1:T(8,128)S(1)} %copy.270, f32[4096]{0:T(1024)S(1)} %fusion.83), kind=kCustom, calls=%fused_computation.77 | custom fusion | flops 49152 | bytes 131632 | tf_op jit(solution)/shard_map/scatter-add | solution.py:76
  117.3 25.4 %scatter_custom_fusion.2 = f32[4,2051]{0,1:T(8,128)S(1)} fusion(f32[4,2051]{0,1:T(8,128)S(1)} %scatter_custom_fusion.1, s32[4096]{0:T(1024)} %get-tuple-element.166, f32[4096]{0:T(1024)S(1)} %get-tuple-element.158, f32[4,4096]{0,1:T(8,128)S(1)} %copy.270, f32[4096]{0:T(1024)S(1)} %fusion.83), kind=kCustom, calls=%fused_computation.75 | custom fusion | flops 49152 | bytes 2162736 | tf_op jit(solution)/shard_map/scatter-add | solution.py:76
  142.6 25.4 %scatter_custom_fusion.3 = f32[4,2051]{0,1:T(8,128)S(1)} fusion(f32[4,2051]{0,1:T(8,128)S(1)} %scatter_custom_fusion.2, s32[4096]{0:T(1024)} %get-tuple-element.167, f32[4096]{0:T(1024)S(1)} %get-tuple-element.157, f32[4,4096]{0,1:T(8,128)S(1)} %copy.270, f32[4096]{0:T(1024)S(1)} %fusion.83), kind=kCustom, calls=%fused_computation.73 | custom fusion | flops 49152 | bytes 2162736 | tf_op jit(solution)/shard_map/scatter-add | solution.py:76
  168.1 25.4 %scatter_custom_fusion.4 = f32[4,2051]{0,1:T(8,128)S(1)} fusion(f32[4,2051]{0,1:T(8,128)S(1)} %scatter_custom_fusion.3, s32[4096]{0:T(1024)S(1)} %get-tuple-element.171, f32[4096]{0:T(1024)S(1)} %get-tuple-element.106, f32[4,4096]{0,1:T(8,128)S(1)} %copy.270, f32[4096]{0:T(1024)S(1)} %fusion.83), kind=kCustom, calls=%fused_computation.71 | custom fusion | flops 49152 | bytes 2162736 | tf_op jit(solution)/shard_map/scatter-add | solution.py:76
  201.3 36.5 %reduce-scatter.10.cloned.1.call-done = f32[256,4]{1,0:T(8,128)} async-done(((f32[2048,4]{1,0:T(8,128)}), f32[256,4]{1,0:T(8,128)}) %reduce-scatter.10.cloned.1.call-update) | async-done | bytes 4112
  282.5 14.1 %gather_fusion.2 = f32[4096,4]{1,0:T(8,128)} fusion(f32[4,2051]{0,1:T(8,128)S(1)} %constant_dynamic-update-slice_fusion, s32[4096]{0:T(1024)S(1)} %get-tuple-element.170), kind=kCustom, calls=%fused_computation.4.clone | custom fusion | bytes 147456 | tf_op jit(solution)/shard_map/jit(_take)/gather | solution.py:68
  321.7 22.8 %scatter_custom_fusion.5 = f32[5,1024]{0,1:T(8,128)S(1)} fusion(s32[4096]{0:T(1024)} %copy-done.35, f32[4096,5]{1,0:T(8,128)} %copy.277, f32[]{:T(128)} %constant.111.clone.1), kind=kCustom, calls=%fused_computation.111 | custom fusion | flops 20480 | bytes 20992 | tf_op jit(solution)/shard_map/scatter-add | solution.py:62
  344.6 17.2 %psum.58 = f32[5,1024]{1,0:T(8,128)S(1)} all-reduce(f32[5,1024]{1,0:T(8,128)S(1)} %copy.278), channel_id=1, replica_groups=mesh['sky'=8,'tm'=4] {'tm'}, use_global_device_ids=true, to_apply=%region_16.19 | all-reduce | flops 5120 | bytes 40960 | tf_op jit(solution)/shard_map/psum | solution.py:108
  363.1 14.1 %gather_fusion.5 = f32[4096,5]{1,0:T(8,128)} fusion(f32[5,1024]{0,1:T(8,128)S(1)} %copy.279, s32[4096]{0:T(1024)S(1)} %get-tuple-element.172), kind=kCustom, calls=%fused_computation.2.clone | custom fusion | bytes 180224 | tf_op jit(solution)/shard_map/jit(_take)/gather | solution.py:82
  379.6 25.3 %scatter_custom_fusion.6 = f32[4,2051]{0,1:T(8,128)S(1)} fusion(s32[4096]{0:T(1024)} %get-tuple-element.168, f32[4096]{0:T(1024)S(1)} %get-tuple-element.156, f32[]{:T(128)} %constant.111.clone.1, f32[4,4096]{0,1:T(8,128)S(1)} %copy.270, f32[4096]{0:T(1024)S(1)} %fusion.83), kind=kCustom, calls=%fused_computation.61 | custom fusion | flops 49152 | bytes 131632 | tf_op jit(solution)/shard_map/scatter-add | solution.py:76
  404.8 25.6 %scatter_custom_fusion.7 = f32[4,2051]{0,1:T(8,128)S(1)} fusion(f32[4,2051]{0,1:T(8,128)S(1)} %scatter_custom_fusion.6, s32[4096]{0:T(1024)} %get-tuple-element.166, f32[4096]{0:T(1024)S(1)} %get-tuple-element.155, f32[4,4096]{0,1:T(8,128)S(1)} %copy.270, f32[4096]{0:T(1024)S(1)} %fusion.83), kind=kCustom, calls=%fused_computation.59 | custom fusion | flops 49152 | bytes 2162736 | tf_op jit(solution)/shard_map/scatter-add | solution.py:76
  430.5 25.4 %scatter_custom_fusion.8 = f32[4,2051]{0,1:T(8,128)S(1)} fusion(f32[4,2051]{0,1:T(8,128)S(1)} %scatter_custom_fusion.7, s32[4096]{0:T(1024)} %get-tuple-element.167, f32[4096]{0:T(1024)S(1)} %get-tuple-element.154, f32[4,4096]{0,1:T(8,128)S(1)} %copy.270, f32[4096]{0:T(1024)S(1)} %fusion.83), kind=kCustom, calls=%fused_computation.57 | custom fusion | flops 49152 | bytes 2162736 | tf_op jit(solution)/shard_map/scatter-add | solution.py:76
  455.8 25.4 %scatter_custom_fusion.9 = f32[4,2051]{0,1:T(8,128)S(1)} fusion(f32[4,2051]{0,1:T(8,128)S(1)} %scatter_custom_fusion.8, s32[4096]{0:T(1024)} %copy-done.36, f32[4096]{0:T(1024)S(1)} %get-tuple-element.95, f32[4,4096]{0,1:T(8,128)S(1)} %copy.270, f32[4096]{0:T(1024)S(1)} %fusion.83), kind=kCustom, calls=%fused_computation.55 | custom fusion | flops 49152 | bytes 2162736 | tf_op jit(solution)/shard_map/scatter-add | solution.py:76
  487.6 36.2 %reduce-scatter.12.cloned.1.call-done = f32[256,4]{1,0:T(8,128)} async-done(((f32[2048,4]{1,0:T(8,128)}), f32[256,4]{1,0:T(8,128)}) %reduce-scatter.12.cloned.1.call-update) | async-done | bytes 4112
  525.4 39.5 %all-reduce = (f32[]{:T(128)}, f32[]{:T(128)}) all-reduce(f32[]{:T(128)} %get-tuple-element.72, f32[]{:T(128)} %get-tuple-element.71), channel_id=1, replica_groups=mesh['sky'=8,'tm'=4] {'sky','tm'}, use_global_device_ids=true, to_apply=%region_10.12 | all-reduce | flops 2 | bytes 16 | tf_op jit(solution)/shard_map/psum | solution.py:123
  566.7 41.3 %psum.60 = f32[]{:T(128)} all-reduce(f32[]{:T(128)} %multiply_reduce_fusion.1), channel_id=1, replica_groups=mesh['sky'=8,'tm'=4] {'sky','tm'}, use_global_device_ids=true, to_apply=%region_26.29 | all-reduce | flops 1 | bytes 8 | tf_op jit(solution)/shard_map/psum | solution.py:123
  653.3 14.1 %gather_fusion.7 = f32[4096,4]{1,0:T(8,128)} fusion(f32[4,2051]{0,1:T(8,128)S(1)} %copy.282, s32[4096]{0:T(1024)S(1)} %get-tuple-element.170), kind=kCustom, calls=%fused_computation.8.clone | custom fusion | bytes 147456 | tf_op jit(solution)/shard_map/jit(_take)/gather | solution.py:68
  693.1 22.8 %scatter_custom_fusion.10 = f32[5,1024]{0,1:T(8,128)S(1)} fusion(s32[4096]{0:T(1024)} %copy-done.35, f32[4096,5]{1,0:T(8,128)} %copy.286, f32[]{:T(128)} %constant.111.clone.1), kind=kCustom, calls=%fused_computation.109 | custom fusion | flops 20480 | bytes 20992 | tf_op jit(solution)/shard_map/scatter-add | solution.py:62
  716.1 16.2 %psum.61 = f32[5,1024]{1,0:T(8,128)S(1)} all-reduce(f32[5,1024]{1,0:T(8,128)S(1)} %copy.287), channel_id=1, replica_groups=mesh['sky'=8,'tm'=4] {'tm'}, use_global_device_ids=true, to_apply=%region_32.35 | all-reduce | flops 5120 | bytes 40960 | tf_op jit(solution)/shard_map/psum | solution.py:108
  733.6 14.1 %gather_fusion.10 = f32[4096,5]{1,0:T(8,128)} fusion(f32[5,1024]{0,1:T(8,128)S(1)} %copy.288, s32[4096]{0:T(1024)S(1)} %get-tuple-element.172), kind=kCustom, calls=%fused_computation.3.clone | custom fusion | bytes 180224 | tf_op jit(solution)/shard_map/jit(_take)/gather | solution.py:82
  750.0 25.3 %scatter_custom_fusion.11 = f32[4,2051]{0,1:T(8,128)S(1)} fusion(s32[4096]{0:T(1024)} %get-tuple-element.168, f32[4096]{0:T(1024)S(1)} %get-tuple-element.153, f32[]{:T(128)} %constant.111.clone.1, f32[4,4096]{0,1:T(8,128)S(1)} %copy.270, f32[4096]{0:T(1024)S(1)} %fusion.83), kind=kCustom, calls=%fused_computation.45 | custom fusion | flops 49152 | bytes 131632 | tf_op jit(solution)/shard_map/scatter-add | solution.py:76
  775.3 25.4 %scatter_custom_fusion.12 = f32[4,2051]{0,1:T(8,128)S(1)} fusion(f32[4,2051]{0,1:T(8,128)S(1)} %scatter_custom_fusion.11, s32[4096]{0:T(1024)} %get-tuple-element.166, f32[4096]{0:T(1024)S(1)} %get-tuple-element.152, f32[4,4096]{0,1:T(8,128)S(1)} %copy.270, f32[4096]{0:T(1024)S(1)} %fusion.83), kind=kCustom, calls=%fused_computation.43 | custom fusion | flops 49152 | bytes 2162736 | tf_op jit(solution)/shard_map/scatter-add | solution.py:76
  800.7 25.4 %scatter_custom_fusion.13 = f32[4,2051]{0,1:T(8,128)S(1)} fusion(f32[4,2051]{0,1:T(8,128)S(1)} %scatter_custom_fusion.12, s32[4096]{0:T(1024)} %get-tuple-element.167, f32[4096]{0:T(1024)S(1)} %get-tuple-element.151, f32[4,4096]{0,1:T(8,128)S(1)} %copy.270, f32[4096]{0:T(1024)S(1)} %fusion.83), kind=kCustom, calls=%fused_computation.41 | custom fusion | flops 49152 | bytes 2162736 | tf_op jit(solution)/shard_map/scatter-add | solution.py:76
  826.1 25.6 %scatter_custom_fusion.14 = f32[4,2051]{0,1:T(8,128)S(1)} fusion(f32[4,2051]{0,1:T(8,128)S(1)} %scatter_custom_fusion.13, s32[4096]{0:T(1024)} %copy-done.36, f32[4096]{0:T(1024)S(1)} %get-tuple-element.84, f32[4,4096]{0,1:T(8,128)S(1)} %copy.270, f32[4096]{0:T(1024)S(1)} %fusion.83), kind=kCustom, calls=%fused_computation.39 | custom fusion | flops 49152 | bytes 2162736 | tf_op jit(solution)/shard_map/scatter-add | solution.py:76
  857.5 36.8 %reduce-scatter.14.cloned.1.call-done = f32[256,4]{1,0:T(8,128)} async-done(((f32[2048,4]{1,0:T(8,128)}), f32[256,4]{1,0:T(8,128)}) %reduce-scatter.14.cloned.1.call-update) | async-done | bytes 4112
  896.0 39.4 %psum.62 = f32[]{:T(128)} all-reduce(f32[]{:T(128)} %multiply_reduce_fusion), channel_id=1, replica_groups=mesh['sky'=8,'tm'=4] {'sky','tm'}, use_global_device_ids=true, to_apply=%region_40.43 | all-reduce | flops 1 | bytes 8 | tf_op jit(solution)/shard_map/psum | solution.py:134
  982.0 14.1 %gather_fusion.12 = f32[4096,4]{1,0:T(8,128)} fusion(f32[4,2051]{0,1:T(8,128)S(1)} %copy.291, s32[4096]{0:T(1024)S(1)} %get-tuple-element.170), kind=kCustom, calls=%fused_computation.12.clone | custom fusion | bytes 147456 | tf_op jit(solution)/shard_map/jit(_take)/gather | solution.py:68
  1019.8 22.6 %scatter_custom_fusion.15 = f32[5,1024]{0,1:T(8,128)S(1)} fusion(s32[4096]{0:T(1024)} %copy-done.35, f32[4096,5]{1,0:T(8,128)S(1)} %copy.295, f32[]{:T(128)} %constant.111.clone.1), kind=kCustom, calls=%fused_computation.107 | custom fusion | flops 20480 | bytes 20992 | tf_op jit(solution)/shard_map/scatter-add | solution.py:62
  1042.6 17.2 %psum.63 = f32[5,1024]{1,0:T(8,128)S(1)} all-reduce(f32[5,1024]{1,0:T(8,128)S(1)} %copy.296), channel_id=1, replica_groups=mesh['sky'=8,'tm'=4] {'tm'}, use_global_device_ids=true, to_apply=%region_46.49 | all-reduce | flops 5120 | bytes 40960 | tf_op jit(solution)/shard_map/psum | solution.py:108
  (193 shorter events, 253.3 us)
Async XLA Ops:
  7.2 65.2 %all-reduce.3.cloned.1.call-start = ((), (), s32[]{:S(2)}) async-start(), calls=%async_computation.3 | async-start | bytes 196608 | tf_op jit(solution)/shard_map/psum | solution.py:101
  11.7 60.7 %copy-start.34 = (f32[5,1024]{1,0:T(8,128)S(1)}, f32[5,1024]{1,0:T(8,128)}, u32[]{:S(2)}) copy-start(f32[5,1024]{1,0:T(8,128)} %param.25) | copy-start | bytes 61444
  35.0 202.8 %reduce-scatter.10.cloned.1.call-start = ((), (), s32[]{:S(2)}) async-start(), calls=%async_computation.4 | async-start | bytes 1179648
  35.7 132.3 %copy-start.36 = (s32[4096]{0:T(1024)}, s32[4096]{0:T(1024)S(1)}, u32[]{:S(2)}) copy-start(s32[4096]{0:T(1024)S(1)} %get-tuple-element.171) | copy-start | bytes 49156
  35.7 343.7 %copy-start.21 = (pred[4096]{0:T(1024)(128)(4,1)}, pred[4096]{0:T(1024)(128)(4,1)S(1)}, u32[]{:S(2)}) copy-start(pred[4096]{0:T(1024)(128)(4,1)S(1)} %compare_and_fusion.4) | copy-start | bytes 12292
  73.6 288.4 %copy-start.3 = (f32[1,1024]{1,0:T(1,128)}, f32[1,1024]{1,0:T(1,128)S(1)}, u32[]{:S(2)}) copy-start(f32[1,1024]{1,0:T(1,128)S(1)} %get-tuple-element.128) | copy-start | bytes 12292
  73.6 288.4 %copy-start.5 = (f32[1,1024]{1,0:T(1,128)}, f32[1,1024]{1,0:T(1,128)S(1)}, u32[]{:S(2)}) copy-start(f32[1,1024]{1,0:T(1,128)S(1)} %get-tuple-element.129) | copy-start | bytes 12292
  73.6 288.4 %copy-start.7 = (f32[1,1024]{1,0:T(1,128)}, f32[1,1024]{1,0:T(1,128)S(1)}, u32[]{:S(2)}) copy-start(f32[1,1024]{1,0:T(1,128)S(1)} %get-tuple-element.130) | copy-start | bytes 12292
  194.6 4.6 collective-permute-start
  201.2 322.6 %reduce-scatter.12.cloned.1.call-start = ((), (), s32[]{:S(2)}) async-start(), calls=%async_computation.5 | async-start | bytes 1179648
  201.3 109.3 %copy-start.13 = (pred[4096]{0:T(1024)(128)(4,1)}, pred[4096]{0:T(1024)(128)(4,1)S(1)}, u32[]{:S(2)}) copy-start(pred[4096]{0:T(1024)(128)(4,1)S(1)} %get-tuple-element.160) | copy-start | bytes 12292
  201.3 109.3 %copy-start.15 = (pred[4096]{0:T(1024)(128)(4,1)}, pred[4096]{0:T(1024)(128)(4,1)S(1)}, u32[]{:S(2)}) copy-start(pred[4096]{0:T(1024)(128)(4,1)S(1)} %get-tuple-element.161) | copy-start | bytes 12292
  201.3 109.3 %copy-start.17 = (pred[4096]{0:T(1024)(128)(4,1)}, pred[4096]{0:T(1024)(128)(4,1)S(1)}, u32[]{:S(2)}) copy-start(pred[4096]{0:T(1024)(128)(4,1)S(1)} %get-tuple-element.162) | copy-start | bytes 12292
  201.3 109.3 %copy-start.19 = (pred[4096]{0:T(1024)(128)(4,1)}, pred[4096]{0:T(1024)(128)(4,1)S(1)}, u32[]{:S(2)}) copy-start(pred[4096]{0:T(1024)(128)(4,1)S(1)} %get-tuple-element.163) | copy-start | bytes 12292
  248.8 5.5 collective-permute-start.1
  319.6 42.4 %copy-start.26 = (f32[1,1024]{1,0:T(1,128)S(1)}, f32[1,1024]{1,0:T(1,128)}, u32[]{:S(2)}) copy-start(f32[1,1024]{1,0:T(1,128)} %get-tuple-element.113) | copy-start | bytes 12292
  319.6 42.4 %copy-start.28 = (f32[1,1024]{1,0:T(1,128)S(1)}, f32[1,1024]{1,0:T(1,128)}, u32[]{:S(2)}) copy-start(f32[1,1024]{1,0:T(1,128)} %get-tuple-element.114) | copy-start | bytes 12292
  319.6 42.4 %copy-start.30 = (f32[1,1024]{1,0:T(1,128)S(1)}, f32[1,1024]{1,0:T(1,128)}, u32[]{:S(2)}) copy-start(f32[1,1024]{1,0:T(1,128)} %get-tuple-element.115) | copy-start | bytes 12292
  319.6 42.4 %copy-start.32 = (f32[1,1024]{1,0:T(1,128)S(1)}, f32[1,1024]{1,0:T(1,128)}, u32[]{:S(2)}) copy-start(f32[1,1024]{1,0:T(1,128)} %get-tuple-element.116) | copy-start | bytes 12292
  482.3 2.6 collective-permute-start.2
  487.5 406.9 %reduce-scatter.14.cloned.1.call-start = ((), (), s32[]{:S(2)}) async-start(), calls=%async_computation.6 | async-start | bytes 1179648
  487.6 137.1 %copy-start.11 = (f32[4,256]{1,0:T(4,128)}, f32[4,256]{1,0:T(4,128)S(1)}, u32[]{:S(2)}) copy-start(f32[4,256]{1,0:T(4,128)S(1)} %copy.300) | copy-start | bytes 12292
  619.3 5.5 collective-permute-start.3
  691.0 41.4 %copy-start.27 = (f32[1,1024]{1,0:T(1,128)S(1)}, f32[1,1024]{1,0:T(1,128)}, u32[]{:S(2)}) copy-start(f32[1,1024]{1,0:T(1,128)} %get-tuple-element.113) | copy-start | bytes 12292
  691.0 41.4 %copy-start.29 = (f32[1,1024]{1,0:T(1,128)S(1)}, f32[1,1024]{1,0:T(1,128)}, u32[]{:S(2)}) copy-start(f32[1,1024]{1,0:T(1,128)} %get-tuple-element.114) | copy-start | bytes 12292
  851.6 85.0 %copy-start.12 = (f32[4,256]{1,0:T(4,128)S(1)}, f32[4,256]{1,0:T(4,128)}, u32[]{:S(2)}) copy-start(f32[4,256]{1,0:T(4,128)} %copy-done.11) | copy-start | bytes 12292
  852.7 2.8 collective-permute-start.4
  857.5 152.6 %copy-start.14 = (pred[4096]{0:T(1024)(128)(4,1)S(1)}, pred[4096]{0:T(1024)(128)(4,1)}, u32[]{:S(2)}) copy-start(pred[4096]{0:T(1024)(128)(4,1)} %copy-done.13) | copy-start | bytes 12292
  857.5 152.6 %copy-start.16 = (pred[4096]{0:T(1024)(128)(4,1)S(1)}, pred[4096]{0:T(1024)(128)(4,1)}, u32[]{:S(2)}) copy-start(pred[4096]{0:T(1024)(128)(4,1)} %copy-done.15) | copy-start | bytes 12292
  857.5 152.6 %copy-start.18 = (pred[4096]{0:T(1024)(128)(4,1)S(1)}, pred[4096]{0:T(1024)(128)(4,1)}, u32[]{:S(2)}) copy-start(pred[4096]{0:T(1024)(128)(4,1)} %copy-done.17) | copy-start | bytes 12292
  857.5 152.6 %copy-start.20 = (pred[4096]{0:T(1024)(128)(4,1)S(1)}, pred[4096]{0:T(1024)(128)(4,1)}, u32[]{:S(2)}) copy-start(pred[4096]{0:T(1024)(128)(4,1)} %copy-done.19) | copy-start | bytes 12292
  948.0 5.5 collective-permute-start.5
  (15 other events, 390.2 us)
Sparse Core Ops, SparseCore 0:
  35.1 37.1 all-reduce.2
  201.3 36.4 reduce-scatter.9
  487.6 36.1 reduce-scatter.11
  857.6 36.7 reduce-scatter.13
where the time goes:
time: 1080 us; the launch traced here: 1070 us
  other arithmetic  437 us (40%)
  local copies, waits for them, and re-layouts  238 us (22%)
  blocking collectives  202 us (19%)
  waiting for transfers between devices  161 us (15%)
  between operations  19.3 us (2%)
    scatter-add x12, other arithmetic, knot_total(): summed.at[:, knot + tap_at].add(design * (tap_weights[tap_at] * weight_vec))  305 us
    gather x12, local copies, waits for them, and re-layouts, knot_values(): picked = jnp.take(padded, knot + tap_at, axis=1)  169 us
    unnamed x7, waiting for transfers between devices  110 us
    scatter-add x4, other arithmetic, source_total(): jnp.zeros((rows.shape[0], count), jnp.float32).at[:, source].add(rows)  90.6 us
    psum x2, blocking collectives, norm_sum(): return lax.psum(partial_value, ('sky', 'tm'))  80.7 us
    psum x3, blocking collectives, source_part(): lax.psum(source_total(obs_source, src_rows * values_obs, SRC_DEV), 'tm')  50.7 us
    gather x6, local copies, waits for them, and re-layouts, eliminate(): fitted = jnp.sum(design * jnp.take(solved, source, axis=1), axis=0)  48.9 us
    psum x1, blocking collectives, shards(): alpha_step = norm_now / lax.psum(jnp.sum(direction * mapped), ('sky', 'tm'))  39.4 us
  transfers between devices with their start and end apart: 10, of which 10 were waited for; matrix products, arithmetic and copies ran while one was open for 0% of the time, Pallas kernels for 0%

commit v1 on v0

--- a/solution.py
+++ b/solution.py
@@ -120,7 +120,7 @@
         return lax.psum_scatter(partial_value, "sky", scatter_dimension=1, tiled=True)
 
     def norm_sum(partial_value):
-        return lax.psum(partial_value, ("sky", "tm"))
+        return jnp.sum(lax.all_gather(partial_value, ("sky", "tm")), axis=0)
 
     cleaned = eliminate(factor, obs_source, src_rows, observed, sums[15:])
     residual = back_to_knots(cleaned)

time: 1080 us -> 1080 us (level)
    psum x2 -> x0, blocking collectives: 80.7 us -> none  [norm_sum(): return lax.psum(partial_value, ('sky', 'tm'))]
    unnamed x0 -> x2, blocking collectives: none -> 80.5 us
where the time goes in v1:
time: 1080 us; the launch traced here: 1070 us
  other arithmetic  438 us (41%)
  local copies, waits for them, and re-layouts  240 us (22%)
  blocking collectives  201 us (19%)
  waiting for transfers between devices  161 us (15%)
  between operations  19.4 us (2%)
    scatter-add x12, other arithmetic, knot_total(): summed.at[:, knot + tap_at].add(design * (tap_weights[tap_at] * weight_vec))  305 us
    gather x12, local copies, waits for them, and re-layouts, knot_values(): picked = jnp.take(padded, knot + tap_at, axis=1)  169 us
    unnamed x7, waiting for transfers between devices  110 us
    scatter-add x4, other arithmetic, source_total(): jnp.zeros((rows.shape[0], count), jnp.float32).at[:, source].add(rows)  90.6 us
    unnamed x2, blocking collectives  80.5 us
    psum x3, blocking collectives, source_part(): lax.psum(source_total(obs_source, src_rows * values_obs, SRC_DEV), 'tm')  50.6 us
    gather x6, local copies, waits for them, and re-layouts, eliminate(): fitted = jnp.sum(design * jnp.take(solved, source, axis=1), axis=0)  48.9 us
    psum x1, blocking collectives, shards(): alpha_step = norm_now / lax.psum(jnp.sum(direction * mapped), ('sky', 'tm'))  39.5 us
  transfers between devices with their start and end apart: 10, of which 10 were waited for; matrix products, arithmetic and copies ran while one was open for 0% of the time, Pallas kernels for 0%

profile of v1, /device:TPU:0, one launch (start us, length us, event | category | flops | bytes accessed | tf_op | source)
XLA Modules:
  0.0 1070.4 jit_solution(15198423477817513377)
XLA Ops:
  11.7 22.5 %scatter_custom_fusion = f32[20,1024]{0,1:T(8,128)S(1)} fusion(s32[4096]{0:T(1024)S(1)} %get-tuple-element.173, f32[4096,20]{1,0:T(8,128)S(1)} %copy.271, f32[]{:T(128)} %constant.111.clone.1), kind=kCustom, calls=%fused_computation.113 | custom fusion | flops 81920 | bytes 81924 | tf_op jit(solution)/shard_map/scatter-add | solution.py:62
  37.1 35.3 %all-reduce.5.cloned.1.call-done = f32[20,1024]{1,0:T(8,128)} async-done(((f32[20,1024]{1,0:T(8,128)}), f32[20,1024]{1,0:T(8,128)}) %all-reduce.5.cloned.1.call-update) | async-done | bytes 81936 | tf_op jit(solution)/shard_map/psum | solution.py:101
  75.5 14.1 %gather_fusion = f32[4096,5]{1,0:T(8,128)} fusion(f32[5,1024]{0,1:T(8,128)S(1)} %copy.273, s32[4096]{0:T(1024)S(1)} %get-tuple-element.172), kind=kCustom, calls=%fused_computation.clone | custom fusion | bytes 180224 | tf_op jit(solution)/shard_map/jit(_take)/gather | solution.py:82
  92.0 25.3 %scatter_custom_fusion.1 = f32[4,2051]{0,1:T(8,128)S(1)} fusion(s32[4096]{0:T(1024)} %get-tuple-element.168, f32[4096]{0:T(1024)S(1)} %get-tuple-element.159, f32[]{:T(128)} %constant.111.clone.1, f32[4,4096]{0,1:T(8,128)S(1)} %copy.270, f32[4096]{0:T(1024)S(1)} %fusion.83), kind=kCustom, calls=%fused_computation.77 | custom fusion | flops 49152 | bytes 131632 | tf_op jit(solution)/shard_map/scatter-add | solution.py:76
  117.3 25.4 %scatter_custom_fusion.2 = f32[4,2051]{0,1:T(8,128)S(1)} fusion(f32[4,2051]{0,1:T(8,128)S(1)} %scatter_custom_fusion.1, s32[4096]{0:T(1024)} %get-tuple-element.166, f32[4096]{0:T(1024)S(1)} %get-tuple-element.158, f32[4,4096]{0,1:T(8,128)S(1)} %copy.270, f32[4096]{0:T(1024)S(1)} %fusion.83), kind=kCustom, calls=%fused_computation.75 | custom fusion | flops 49152 | bytes 2162736 | tf_op jit(solution)/shard_map/scatter-add | solution.py:76
  142.6 25.4 %scatter_custom_fusion.3 = f32[4,2051]{0,1:T(8,128)S(1)} fusion(f32[4,2051]{0,1:T(8,128)S(1)} %scatter_custom_fusion.2, s32[4096]{0:T(1024)} %get-tuple-element.167, f32[4096]{0:T(1024)S(1)} %get-tuple-element.157, f32[4,4096]{0,1:T(8,128)S(1)} %copy.270, f32[4096]{0:T(1024)S(1)} %fusion.83), kind=kCustom, calls=%fused_computation.73 | custom fusion | flops 49152 | bytes 2162736 | tf_op jit(solution)/shard_map/scatter-add | solution.py:76
  168.1 25.4 %scatter_custom_fusion.4 = f32[4,2051]{0,1:T(8,128)S(1)} fusion(f32[4,2051]{0,1:T(8,128)S(1)} %scatter_custom_fusion.3, s32[4096]{0:T(1024)S(1)} %get-tuple-element.171, f32[4096]{0:T(1024)S(1)} %get-tuple-element.106, f32[4,4096]{0,1:T(8,128)S(1)} %copy.270, f32[4096]{0:T(1024)S(1)} %fusion.83), kind=kCustom, calls=%fused_computation.71 | custom fusion | flops 49152 | bytes 2162736 | tf_op jit(solution)/shard_map/scatter-add | solution.py:76
  201.3 36.5 %reduce-scatter.10.cloned.1.call-done = f32[256,4]{1,0:T(8,128)} async-done(((f32[2048,4]{1,0:T(8,128)}), f32[256,4]{1,0:T(8,128)}) %reduce-scatter.10.cloned.1.call-update) | async-done | bytes 4112
  321.7 22.8 %scatter_custom_fusion.5 = f32[5,1024]{0,1:T(8,128)S(1)} fusion(s32[4096]{0:T(1024)} %copy-done.35, f32[4096,5]{1,0:T(8,128)} %copy.277, f32[]{:T(128)} %constant.111.clone.1), kind=kCustom, calls=%fused_computation.111 | custom fusion | flops 20480 | bytes 20992 | tf_op jit(solution)/shard_map/scatter-add | solution.py:62
  344.6 17.2 %psum.43 = f32[5,1024]{1,0:T(8,128)S(1)} all-reduce(f32[5,1024]{1,0:T(8,128)S(1)} %copy.278), channel_id=1, replica_groups=mesh['sky'=8,'tm'=4] {'tm'}, use_global_device_ids=true, to_apply=%region_16.19 | all-reduce | flops 5120 | bytes 40960 | tf_op jit(solution)/shard_map/psum | solution.py:108
  363.1 14.1 %gather_fusion.5 = f32[4096,5]{1,0:T(8,128)} fusion(f32[5,1024]{0,1:T(8,128)S(1)} %copy.279, s32[4096]{0:T(1024)S(1)} %get-tuple-element.172), kind=kCustom, calls=%fused_computation.2.clone | custom fusion | bytes 180224 | tf_op jit(solution)/shard_map/jit(_take)/gather | solution.py:82
  379.6 25.3 %scatter_custom_fusion.6 = f32[4,2051]{0,1:T(8,128)S(1)} fusion(s32[4096]{0:T(1024)} %get-tuple-element.168, f32[4096]{0:T(1024)S(1)} %get-tuple-element.156, f32[]{:T(128)} %constant.111.clone.1, f32[4,4096]{0,1:T(8,128)S(1)} %copy.270, f32[4096]{0:T(1024)S(1)} %fusion.83), kind=kCustom, calls=%fused_computation.61 | custom fusion | flops 49152 | bytes 131632 | tf_op jit(solution)/shard_map/scatter-add | solution.py:76
  404.8 25.6 %scatter_custom_fusion.7 = f32[4,2051]{0,1:T(8,128)S(1)} fusion(f32[4,2051]{0,1:T(8,128)S(1)} %scatter_custom_fusion.6, s32[4096]{0:T(1024)} %get-tuple-element.166, f32[4096]{0:T(1024)S(1)} %get-tuple-element.155, f32[4,4096]{0,1:T(8,128)S(1)} %copy.270, f32[4096]{0:T(1024)S(1)} %fusion.83), kind=kCustom, calls=%fused_computation.59 | custom fusion | flops 49152 | bytes 2162736 | tf_op jit(solution)/shard_map/scatter-add | solution.py:76
  430.5 25.4 %scatter_custom_fusion.8 = f32[4,2051]{0,1:T(8,128)S(1)} fusion(f32[4,2051]{0,1:T(8,128)S(1)} %scatter_custom_fusion.7, s32[4096]{0:T(1024)} %get-tuple-element.167, f32[4096]{0:T(1024)S(1)} %get-tuple-element.154, f32[4,4096]{0,1:T(8,128)S(1)} %copy.270, f32[4096]{0:T(1024)S(1)} %fusion.83), kind=kCustom, calls=%fused_computation.57 | custom fusion | flops 49152 | bytes 2162736 | tf_op jit(solution)/shard_map/scatter-add | solution.py:76
  455.8 25.4 %scatter_custom_fusion.9 = f32[4,2051]{0,1:T(8,128)S(1)} fusion(f32[4,2051]{0,1:T(8,128)S(1)} %scatter_custom_fusion.8, s32[4096]{0:T(1024)} %copy-done.36, f32[4096]{0:T(1024)S(1)} %get-tuple-element.95, f32[4,4096]{0,1:T(8,128)S(1)} %copy.270, f32[4096]{0:T(1024)S(1)} %fusion.83), kind=kCustom, calls=%fused_computation.55 | custom fusion | flops 49152 | bytes 2162736 | tf_op jit(solution)/shard_map/scatter-add | solution.py:76
  487.6 36.1 %reduce-scatter.12.cloned.1.call-done = f32[256,4]{1,0:T(8,128)} async-done(((f32[2048,4]{1,0:T(8,128)}), f32[256,4]{1,0:T(8,128)}) %reduce-scatter.12.cloned.1.call-update) | async-done | bytes 4112
  526.1 39.5 %all-reduce.2 = (f32[32]{0:T(128)S(1)}, f32[]{:T(128)}) all-reduce(f32[32]{0:T(128)S(1)} %dynamic-update-slice.9, f32[]{:T(128)} %get-tuple-element.71), channel_id=1, replica_groups=mesh['sky'=8,'tm'=4] {'sky','tm'}, use_global_device_ids=true, to_apply=%add | all-reduce | flops 33 | bytes 264
  568.7 41.1 %all-reduce.1 = f32[32]{0:T(128)S(1)} all-reduce(f32[32]{0:T(128)S(1)} %dynamic-update-slice.10), channel_id=1, replica_groups=mesh['sky'=8,'tm'=4] {'sky','tm'}, use_global_device_ids=true, to_apply=%add.1 | all-reduce | flops 32 | bytes 256
  627.4 14.1 %gather_fusion.6 = f32[4096,4]{1,0:T(8,128)} fusion(f32[4,2051]{0,1:T(8,128)S(1)} %copy.282, s32[4096]{0:T(1024)S(1)} %get-tuple-element.165), kind=kCustom, calls=%fused_computation.7.clone | custom fusion | bytes 147456 | tf_op jit(solution)/shard_map/jit(_take)/gather | solution.py:68
  641.5 14.1 %gather_fusion.7 = f32[4096,4]{1,0:T(8,128)} fusion(f32[4,2051]{0,1:T(8,128)S(1)} %copy.282, s32[4096]{0:T(1024)S(1)} %get-tuple-element.170), kind=kCustom, calls=%fused_computation.8.clone | custom fusion | bytes 147456 | tf_op jit(solution)/shard_map/jit(_take)/gather | solution.py:68
  695.4 22.8 %scatter_custom_fusion.10 = f32[5,1024]{0,1:T(8,128)S(1)} fusion(s32[4096]{0:T(1024)} %copy-done.35, f32[4096,5]{1,0:T(8,128)} %copy.286, f32[]{:T(128)} %constant.111.clone.1), kind=kCustom, calls=%fused_computation.109 | custom fusion | flops 20480 | bytes 20992 | tf_op jit(solution)/shard_map/scatter-add | solution.py:62
  718.3 16.2 %psum.45 = f32[5,1024]{1,0:T(8,128)S(1)} all-reduce(f32[5,1024]{1,0:T(8,128)S(1)} %copy.287), channel_id=1, replica_groups=mesh['sky'=8,'tm'=4] {'tm'}, use_global_device_ids=true, to_apply=%region_32.35 | all-reduce | flops 5120 | bytes 40960 | tf_op jit(solution)/shard_map/psum | solution.py:108
  735.8 14.1 %gather_fusion.10 = f32[4096,5]{1,0:T(8,128)} fusion(f32[5,1024]{0,1:T(8,128)S(1)} %copy.288, s32[4096]{0:T(1024)S(1)} %get-tuple-element.172), kind=kCustom, calls=%fused_computation.3.clone | custom fusion | bytes 180224 | tf_op jit(solution)/shard_map/jit(_take)/gather | solution.py:82
  752.3 25.3 %scatter_custom_fusion.11 = f32[4,2051]{0,1:T(8,128)S(1)} fusion(s32[4096]{0:T(1024)} %get-tuple-element.168, f32[4096]{0:T(1024)S(1)} %get-tuple-element.153, f32[]{:T(128)} %constant.111.clone.1, f32[4,4096]{0,1:T(8,128)S(1)} %copy.270, f32[4096]{0:T(1024)S(1)} %fusion.83), kind=kCustom, calls=%fused_computation.45 | custom fusion | flops 49152 | bytes 131632 | tf_op jit(solution)/shard_map/scatter-add | solution.py:76
  777.5 25.4 %scatter_custom_fusion.12 = f32[4,2051]{0,1:T(8,128)S(1)} fusion(f32[4,2051]{0,1:T(8,128)S(1)} %scatter_custom_fusion.11, s32[4096]{0:T(1024)} %get-tuple-element.166, f32[4096]{0:T(1024)S(1)} %get-tuple-element.152, f32[4,4096]{0,1:T(8,128)S(1)} %copy.270, f32[4096]{0:T(1024)S(1)} %fusion.83), kind=kCustom, calls=%fused_computation.43 | custom fusion | flops 49152 | bytes 2162736 | tf_op jit(solution)/shard_map/scatter-add | solution.py:76
  802.9 25.4 %scatter_custom_fusion.13 = f32[4,2051]{0,1:T(8,128)S(1)} fusion(f32[4,2051]{0,1:T(8,128)S(1)} %scatter_custom_fusion.12, s32[4096]{0:T(1024)} %get-tuple-element.167, f32[4096]{0:T(1024)S(1)} %get-tuple-element.151, f32[4,4096]{0,1:T(8,128)S(1)} %copy.270, f32[4096]{0:T(1024)S(1)} %fusion.83), kind=kCustom, calls=%fused_computation.41 | custom fusion | flops 49152 | bytes 2162736 | tf_op jit(solution)/shard_map/scatter-add | solution.py:76
  828.3 25.6 %scatter_custom_fusion.14 = f32[4,2051]{0,1:T(8,128)S(1)} fusion(f32[4,2051]{0,1:T(8,128)S(1)} %scatter_custom_fusion.13, s32[4096]{0:T(1024)} %copy-done.36, f32[4096]{0:T(1024)S(1)} %get-tuple-element.84, f32[4,4096]{0,1:T(8,128)S(1)} %copy.270, f32[4096]{0:T(1024)S(1)} %fusion.83), kind=kCustom, calls=%fused_computation.39 | custom fusion | flops 49152 | bytes 2162736 | tf_op jit(solution)/shard_map/scatter-add | solution.py:76
  859.8 36.9 %reduce-scatter.14.cloned.1.call-done = f32[256,4]{1,0:T(8,128)} async-done(((f32[2048,4]{1,0:T(8,128)}), f32[256,4]{1,0:T(8,128)}) %reduce-scatter.14.cloned.1.call-update) | async-done | bytes 4112
  898.2 39.5 %psum.46 = f32[]{:T(128)} all-reduce(f32[]{:T(128)} %multiply_reduce_fusion), channel_id=1, replica_groups=mesh['sky'=8,'tm'=4] {'sky','tm'}, use_global_device_ids=true, to_apply=%region_40.43 | all-reduce | flops 1 | bytes 8 | tf_op jit(solution)/shard_map/psum | solution.py:134
  956.2 14.1 %gather_fusion.11 = f32[4096,4]{1,0:T(8,128)} fusion(f32[4,2051]{0,1:T(8,128)S(1)} %copy.291, s32[4096]{0:T(1024)S(1)} %get-tuple-element.165), kind=kCustom, calls=%fused_computation.11.clone | custom fusion | bytes 147456 | tf_op jit(solution)/shard_map/jit(_take)/gather | solution.py:68
  1022.2 22.6 %scatter_custom_fusion.15 = f32[5,1024]{0,1:T(8,128)S(1)} fusion(s32[4096]{0:T(1024)} %copy-done.35, f32[4096,5]{1,0:T(8,128)S(1)} %copy.295, f32[]{:T(128)} %constant.111.clone.1), kind=kCustom, calls=%fused_computation.107 | custom fusion | flops 20480 | bytes 20992 | tf_op jit(solution)/shard_map/scatter-add | solution.py:62
  1045.0 17.1 %psum.47 = f32[5,1024]{1,0:T(8,128)S(1)} all-reduce(f32[5,1024]{1,0:T(8,128)S(1)} %copy.296), channel_id=1, replica_groups=mesh['sky'=8,'tm'=4] {'tm'}, use_global_device_ids=true, to_apply=%region_46.49 | all-reduce | flops 5120 | bytes 40960 | tf_op jit(solution)/shard_map/psum | solution.py:108
  (199 shorter events, 255.7 us)
Async XLA Ops:
  7.2 65.2 %all-reduce.5.cloned.1.call-start = ((), (), s32[]{:S(2)}) async-start(), calls=%async_computation.3 | async-start | bytes 196608 | tf_op jit(solution)/shard_map/psum | solution.py:101
  11.7 60.7 %copy-start.34 = (f32[5,1024]{1,0:T(8,128)S(1)}, f32[5,1024]{1,0:T(8,128)}, u32[]{:S(2)}) copy-start(f32[5,1024]{1,0:T(8,128)} %param.25) | copy-start | bytes 61444
  35.0 202.8 %reduce-scatter.10.cloned.1.call-start = ((), (), s32[]{:S(2)}) async-start(), calls=%async_computation.4 | async-start | bytes 1179648
  35.7 132.3 %copy-start.36 = (s32[4096]{0:T(1024)}, s32[4096]{0:T(1024)S(1)}, u32[]{:S(2)}) copy-start(s32[4096]{0:T(1024)S(1)} %get-tuple-element.171) | copy-start | bytes 49156
  35.7 343.7 %copy-start.21 = (pred[4096]{0:T(1024)(128)(4,1)}, pred[4096]{0:T(1024)(128)(4,1)S(1)}, u32[]{:S(2)}) copy-start(pred[4096]{0:T(1024)(128)(4,1)S(1)} %compare_and_fusion.4) | copy-start | bytes 12292
  73.6 288.4 %copy-start.3 = (f32[1,1024]{1,0:T(1,128)}, f32[1,1024]{1,0:T(1,128)S(1)}, u32[]{:S(2)}) copy-start(f32[1,1024]{1,0:T(1,128)S(1)} %get-tuple-element.128) | copy-start | bytes 12292
  73.6 288.4 %copy-start.5 = (f32[1,1024]{1,0:T(1,128)}, f32[1,1024]{1,0:T(1,128)S(1)}, u32[]{:S(2)}) copy-start(f32[1,1024]{1,0:T(1,128)S(1)} %get-tuple-element.129) | copy-start | bytes 12292
  73.6 288.4 %copy-start.7 = (f32[1,1024]{1,0:T(1,128)}, f32[1,1024]{1,0:T(1,128)S(1)}, u32[]{:S(2)}) copy-start(f32[1,1024]{1,0:T(1,128)S(1)} %get-tuple-element.130) | copy-start | bytes 12292
  194.6 4.6 collective-permute-start
  201.2 322.6 %reduce-scatter.12.cloned.1.call-start = ((), (), s32[]{:S(2)}) async-start(), calls=%async_computation.5 | async-start | bytes 1179648
  201.3 109.3 %copy-start.13 = (pred[4096]{0:T(1024)(128)(4,1)}, pred[4096]{0:T(1024)(128)(4,1)S(1)}, u32[]{:S(2)}) copy-start(pred[4096]{0:T(1024)(128)(4,1)S(1)} %get-tuple-element.160) | copy-start | bytes 12292
  201.3 109.3 %copy-start.15 = (pred[4096]{0:T(1024)(128)(4,1)}, pred[4096]{0:T(1024)(128)(4,1)S(1)}, u32[]{:S(2)}) copy-start(pred[4096]{0:T(1024)(128)(4,1)S(1)} %get-tuple-element.161) | copy-start | bytes 12292
  201.3 109.3 %copy-start.17 = (pred[4096]{0:T(1024)(128)(4,1)}, pred[4096]{0:T(1024)(128)(4,1)S(1)}, u32[]{:S(2)}) copy-start(pred[4096]{0:T(1024)(128)(4,1)S(1)} %get-tuple-element.162) | copy-start | bytes 12292
  201.3 109.3 %copy-start.19 = (pred[4096]{0:T(1024)(128)(4,1)}, pred[4096]{0:T(1024)(128)(4,1)S(1)}, u32[]{:S(2)}) copy-start(pred[4096]{0:T(1024)(128)(4,1)S(1)} %get-tuple-element.163) | copy-start | bytes 12292
  248.8 5.5 collective-permute-start.1
  319.6 42.4 %copy-start.26 = (f32[1,1024]{1,0:T(1,128)S(1)}, f32[1,1024]{1,0:T(1,128)}, u32[]{:S(2)}) copy-start(f32[1,1024]{1,0:T(1,128)} %get-tuple-element.113) | copy-start | bytes 12292
  319.6 42.4 %copy-start.28 = (f32[1,1024]{1,0:T(1,128)S(1)}, f32[1,1024]{1,0:T(1,128)}, u32[]{:S(2)}) copy-start(f32[1,1024]{1,0:T(1,128)} %get-tuple-element.114) | copy-start | bytes 12292
  319.6 42.4 %copy-start.30 = (f32[1,1024]{1,0:T(1,128)S(1)}, f32[1,1024]{1,0:T(1,128)}, u32[]{:S(2)}) copy-start(f32[1,1024]{1,0:T(1,128)} %get-tuple-element.115) | copy-start | bytes 12292
  319.6 42.4 %copy-start.32 = (f32[1,1024]{1,0:T(1,128)S(1)}, f32[1,1024]{1,0:T(1,128)}, u32[]{:S(2)}) copy-start(f32[1,1024]{1,0:T(1,128)} %get-tuple-element.116) | copy-start | bytes 12292
  482.3 2.6 collective-permute-start.2
  487.5 409.2 %reduce-scatter.14.cloned.1.call-start = ((), (), s32[]{:S(2)}) async-start(), calls=%async_computation.6 | async-start | bytes 1179648
  487.6 139.4 %copy-start.11 = (f32[4,256]{1,0:T(4,128)}, f32[4,256]{1,0:T(4,128)S(1)}, u32[]{:S(2)}) copy-start(f32[4,256]{1,0:T(4,128)S(1)} %copy.300) | copy-start | bytes 12292
  621.6 5.5 collective-permute-start.3
  693.3 41.4 %copy-start.27 = (f32[1,1024]{1,0:T(1,128)S(1)}, f32[1,1024]{1,0:T(1,128)}, u32[]{:S(2)}) copy-start(f32[1,1024]{1,0:T(1,128)} %get-tuple-element.113) | copy-start | bytes 12292
  693.3 41.4 %copy-start.29 = (f32[1,1024]{1,0:T(1,128)S(1)}, f32[1,1024]{1,0:T(1,128)}, u32[]{:S(2)}) copy-start(f32[1,1024]{1,0:T(1,128)} %get-tuple-element.114) | copy-start | bytes 12292
  853.9 85.1 %copy-start.12 = (f32[4,256]{1,0:T(4,128)S(1)}, f32[4,256]{1,0:T(4,128)}, u32[]{:S(2)}) copy-start(f32[4,256]{1,0:T(4,128)} %copy-done.11) | copy-start | bytes 12292
  855.0 2.8 collective-permute-start.4
  859.7 152.7 %copy-start.14 = (pred[4096]{0:T(1024)(128)(4,1)S(1)}, pred[4096]{0:T(1024)(128)(4,1)}, u32[]{:S(2)}) copy-start(pred[4096]{0:T(1024)(128)(4,1)} %copy-done.13) | copy-start | bytes 12292
  859.8 152.7 %copy-start.16 = (pred[4096]{0:T(1024)(128)(4,1)S(1)}, pred[4096]{0:T(1024)(128)(4,1)}, u32[]{:S(2)}) copy-start(pred[4096]{0:T(1024)(128)(4,1)} %copy-done.15) | copy-start | bytes 12292
  859.8 152.7 %copy-start.18 = (pred[4096]{0:T(1024)(128)(4,1)S(1)}, pred[4096]{0:T(1024)(128)(4,1)}, u32[]{:S(2)}) copy-start(pred[4096]{0:T(1024)(128)(4,1)} %copy-done.17) | copy-start | bytes 12292
  859.8 152.7 %copy-start.20 = (pred[4096]{0:T(1024)(128)(4,1)S(1)}, pred[4096]{0:T(1024)(128)(4,1)}, u32[]{:S(2)}) copy-start(pred[4096]{0:T(1024)(128)(4,1)} %copy-done.19) | copy-start | bytes 12292
  950.3 5.5 collective-permute-start.5
  (15 other events, 390.2 us)
Sparse Core Ops, SparseCore 0:
  35.1 37.1 all-reduce.4
  201.3 36.4 reduce-scatter.9
  487.6 36.1 reduce-scatter.11
  859.9 36.7 reduce-scatter.13
